TPU v7x, 32 devices: a 4x2x2 block of a 4x4x8 slice. The times are simulated.
32 devices in a mesh: dp: 4 (over y, z), cp: 8 (over x, core).
Axes of the slice: x: 4, y: 2, z: 2, core: 2. Of those that a mesh axis runs over, the one named last changes fastest.
The devices are a block of a 4x4x8 slice.
Arguments:
- x_in: bfloat16 [32, 2048, 1152], P('dp', 'cp'), parts along dimension 0
- positions: int32 [32, 2048], P('dp', 'cp'), parts along dimension 0
- dy_out: bfloat16 [32, 2048, 1152], P('dp', 'cp'), parts along dimension 0
- w_query: bfloat16 [1152, 4, 256], replicated
- w_key: bfloat16 [1152, 1, 256], replicated
- w_value: bfloat16 [1152, 1, 256], replicated
- w_out: bfloat16 [4, 256, 1152], replicated
- w_pre: float32 [1152], replicated
- w_post: float32 [1152], replicated
Outputs:
- output 1: bfloat16 [32, 2048, 1152], P('dp', 'cp'), parts along dimension 0
- output 2: bfloat16 [32, 2048, 1152], P('dp', 'cp'), parts along dimension 0
- output 3: float32 [4608, 4, 256], P('dp'), parts along dimension 0
- output 4: float32 [4608, 1, 256], P('dp'), parts along dimension 0
- output 5: float32 [4608, 1, 256], P('dp'), parts along dimension 0
- output 6: float32 [16, 256, 1152], P('dp'), parts along dimension 0
- output 7: float32 [4608], P('dp'), parts along dimension 0
- output 8: float32 [4608], P('dp'), parts along dimension 0
There are 4 independent parts. A program takes and returns all parts, laid end to end along the dimension named above; an argument that names none is the same for every part.
All inputs are finite; a program needn't handle non-finite values.
Results may differ from a plain program's by a relative error of at most 0.02.
Values are sent between devices in bfloat16 or wider.
A program may use at most 768 MiB of HBM per device.

v0:
```python
import functools

import jax
import jax.numpy as jnp
from jax import lax
from jax.experimental import pallas as pl
from jax.experimental.pallas import tpu as pltpu
from jax.sharding import PartitionSpec as P

NORM_EPS = 1e-6
SOFT_CAP = 50.0
QUERY_SCALE = 144.0
ROPE_BASE = 10000.0

NN = (((1,), (0,)), ((), ()))
NT = (((1,), (1,)), ((), ()))
TN = (((0,), (0,)), ((), ()))

def dot(a, b, dims=NN):
    return lax.dot_general(a, b, dims, preferred_element_type=jnp.float32)


def rope_tables(positions, head_dim):
    half = head_dim // 2
    inv_freq = ROPE_BASE ** (jnp.arange(half, dtype=jnp.float32) * (-2.0 / head_dim))
    angles = positions.astype(jnp.float32)[:, :, None] * inv_freq
    return jnp.cos(angles), jnp.sin(angles)


def rotate(values, cosine, sine):
    half = values.shape[-1] // 2
    first = values[..., :half]
    second = values[..., half:]
    return jnp.concatenate([first * cosine - second * sine, second * cosine + first * sine], axis=-1)


def rotate_back(values, cosine, sine):
    half = values.shape[-1] // 2
    first = values[..., :half]
    second = values[..., half:]
    return jnp.concatenate([first * cosine + second * sine, second * cosine - first * sine], axis=-1)


def bf(values):
    return values.astype(jnp.bfloat16)


def inv_rms(values):
    return lax.rsqrt(jnp.mean(values * values, axis=-1, keepdims=True) + NORM_EPS)


def norm_grad(u, gain, cot):
    r = inv_rms(u)
    g = cot * (1.0 + gain)
    du = r * g - u * (r * r * r) * jnp.mean(g * u, axis=-1, keepdims=True)
    return du, cot * (u * r)


MESH = pl.DeviceIdType.MESH


def at(ref, i, n):
    return ref.at[:, pl.ds(pl.multiple_of(i * n, n), n)]


def greet(me, count):
    barrier = pltpu.get_barrier_semaphore()
    for step in range(1, count):
        pl.semaphore_signal(barrier, inc=1, device_id={"cp": lax.rem(me + step, count)}, device_id_type=MESH)
    pl.semaphore_wait(barrier, count - 1)


def near_first(count):
    return [step for pair in zip(range(1, count // 2 + 1), range(count - 1, count // 2 - 1, -1)) for step in pair][:count - 1]


def distance(t, count):
    return jnp.where(lax.rem(t, 2) == 1, (t + 1) // 2, lax.rem(count - t // 2, count))


class Exchange:
    def __init__(self, src, dst, send_sem, recv_sem, me, count):
        self.src, self.dst, self.send_sem, self.recv_sem, self.me, self.count = src, dst, send_sem, recv_sem, me, count

    def copy(self, step):
        to = lax.rem(self.me + step, self.count)
        return pltpu.make_async_remote_copy(
            src_ref=self.src.at[to], dst_ref=self.dst.at[self.me], send_sem=self.send_sem.at[to],
            recv_sem=self.recv_sem.at[self.me], device_id={"cp": to}, device_id_type=MESH)

    def own(self):
        return pltpu.make_async_copy(self.src.at[self.me], self.dst.at[self.me], self.recv_sem.at[self.me])

    def start(self, steps):
        for step in steps:
            if step:
                self.copy(step).start()
            else:
                self.own().start()

    def wait_from(self, source):
        pltpu.make_async_copy(self.dst.at[source], self.dst.at[source], self.recv_sem.at[source]).wait()

    def wait_sent(self):
        for step in near_first(self.count):
            self.copy(step).wait_send()


def front_kernel(count, heads, x_in, dy_in, angle, gain_pre, gain_post, wq_in, wk_in, wv_in, wo_in,
                 x_out, dy_out, cos_out, sin_out, actt_out, q_out, k_out, kt_out, v_out, y_out, do_out, dwo_out, lse_out, delta_out, dpost_out,
                 x, dy, wq, wk, wv, wo, cosine, sine, actt, q, k, kt, v, vt, of, ot, z, do, dwo, acc, stat,
                 x_send, x_recv, dy_send, dy_recv, w_sem, out_sem, dwo_sem):
    me = lax.axis_index("cp")
    rows, model = x.shape[1:]
    dim = k.shape[-1]
    width = heads * dim
    greet(me, count)
    x_move = Exchange(x_in, x, x_send, x_recv, me, count)
    dy_move = Exchange(dy_in, dy, dy_send, dy_recv, me, count)
    x_move.start(near_first(count) + [0])
    loads = [pltpu.make_async_copy(a, b, w_sem.at[n]) for n, (a, b) in enumerate(((wq_in, wq), (wk_in, wk), (wv_in, wv), (wo_in, wo)))]
    for load in loads:
        load.start()

    def tables(j, carry):
        cosine[j] = jnp.cos(angle[j])
        sine[j] = jnp.sin(angle[j])
        return carry

    lax.fori_loop(0, count, tables, 0)
    for load in loads:
        load.wait()

    def pre(t, carry):
        j = lax.rem(me + count - distance(t, count), count)
        x_move.wait_from(j)

        @pl.when(t == count - 1)
        def _():
            dy_move.start(near_first(count) + [0])

        xf = x[j].astype(jnp.float32)
        act = xf * inv_rms(xf) * (1.0 + gain_pre[...])
        at(actt, j, rows)[...] = bf(act.T)
        act = bf(act)
        c, s = cosine[j], sine[j]
        for h in range(heads):
            cols = slice(h * dim, (h + 1) * dim)
            qh = bf(dot(act, wq[:, cols])).astype(jnp.float32)
            q[j, :, cols] = bf(rotate(qh, c, s) * QUERY_SCALE ** -0.5)
        kh = rotate(bf(dot(act, wk[...])).astype(jnp.float32), c, s)
        k[j] = bf(kh)
        kt[j] = bf(kh.T)
        vh = dot(act, wv[...])
        v[j] = bf(vh)
        vt[j] = bf(vh.T)
        return carry

    lax.fori_loop(0, count, pre, 0)
    early = [pltpu.make_async_copy(a, b, out_sem.at[n]) for n, (a, b) in enumerate(
        ((x, x_out), (cosine, cos_out), (sine, sin_out), (actt, actt_out), (q, q_out), (k, k_out), (kt, kt_out), (v, v_out)))]
    for copy in early:
        copy.start()
    early[0].wait()

    def attend(i, carry):
        acc[...] = jnp.zeros_like(acc)
        stat[0] = jnp.full(stat.shape[1:], -1e30, jnp.float32)
        stat[1] = jnp.zeros(stat.shape[1:], jnp.float32)

        def block(j, masked):
            key, val_t = k[j], vt[j]
            for h in range(heads):
                s = dot(key, q[i, :, h * dim:(h + 1) * dim], NT)
                c = SOFT_CAP * jnp.tanh(s * (1.0 / SOFT_CAP))
                if masked:
                    allowed = lax.broadcasted_iota(jnp.int32, s.shape, 0) <= lax.broadcasted_iota(jnp.int32, s.shape, 1)
                    c = jnp.where(allowed, c, -1e30)
                old = stat[0, h:h + 1, :]
                new = jnp.maximum(old, jnp.max(c, axis=0, keepdims=True))
                scale = jnp.exp(old - new)
                p = jnp.exp(c - new)
                stat[1, h:h + 1, :] = stat[1, h:h + 1, :] * scale + jnp.sum(p, axis=0, keepdims=True)
                stat[0, h:h + 1, :] = new
                acc[h] = acc[h] * scale + dot(val_t, bf(p))

        def body(j, carry):
            block(j, False)
            return carry

        lax.fori_loop(0, i, body, 0)
        block(i, True)
        lse_out[i] = stat[0] + jnp.log(stat[1])
        parts = []
        for h in range(heads):
            out_t = acc[h] / stat[1, h:h + 1, :]
            at(ot.at[h * dim:(h + 1) * dim], i, rows)[...] = bf(out_t)
            out = out_t.T
            of[i, :, h * dim:(h + 1) * dim] = out
            parts.append(bf(out))
        zb = bf(dot(jnp.concatenate(parts, axis=1), wo[...]))
        z[pl.ds(pl.multiple_of(i * rows, rows), rows), :] = zb
        zf = zb.astype(jnp.float32)
        post = bf(zf * inv_rms(zf) * (1.0 + gain_post[...]))
        x[i] = bf(x[i].astype(jnp.float32) + post.astype(jnp.float32))
        return carry

    lax.fori_loop(0, count, attend, 0)
    y_copy = pltpu.make_async_copy(x, y_out, out_sem.at[8])
    y_copy.start()
    dpost_out[...] = jnp.zeros_like(dpost_out)

    def mid(t, carry):
        j = lax.rem(me + count - distance(t, count), count)
        dy_move.wait_from(j)
        rws = pl.ds(pl.multiple_of(j * rows, rows), rows)
        dz, dgain = norm_grad(z[rws, :].astype(jnp.float32), gain_post[...], dy[j].astype(jnp.float32))
        dpost_out[...] += jnp.sum(dgain.reshape(rows // 8, 8, model), axis=0)
        dz = bf(dz)
        z[rws, :] = dz
        lane = lax.broadcasted_iota(jnp.int32, (rows, 128), 1)
        cols = jnp.zeros((rows, 128), jnp.float32)
        for h in range(heads):
            sl = slice(h * dim, (h + 1) * dim)
            doh = bf(dot(dz, wo[sl, :], NT))
            do[j, :, sl] = doh
            cols = jnp.where(lane == h, jnp.sum(doh.astype(jnp.float32) * of[j, :, sl], axis=-1, keepdims=True), cols)
        delta_out[j] = cols.T[:8, :]
        return carry

    lax.fori_loop(0, count, mid, 0)
    late = [pltpu.make_async_copy(dy, dy_out, out_sem.at[9]), pltpu.make_async_copy(do, do_out, out_sem.at[10])]
    for copy in late:
        copy.start()

    def put(h, slot):
        return pltpu.make_async_copy(dwo.at[slot], dwo_out.at[h], dwo_sem.at[slot])

    def weight(h, carry):
        slot = lax.rem(h, 2)

        @pl.when(h >= 2)
        def _():
            put(h - 2, slot).wait()

        dwo[slot] = dot(ot[pl.ds(pl.multiple_of(h * dim, dim), dim), :], z[...])
        put(h, slot).start()
        return carry

    lax.fori_loop(0, heads, weight, 0)
    for h in range(heads - 2, heads):
        put(h, h % 2).wait()
    for copy in early[1:] + [y_copy] + late:
        copy.wait()
    x_move.wait_sent()
    dy_move.wait_sent()


def front(count, heads, x_in, dy_in, angle, gain_pre, gain_post, wq, wk, wv, wo):
    bf16, f32 = jnp.bfloat16, jnp.float32
    _, rows, model = x_in.shape
    dim = wk.shape[1]
    width = heads * dim
    tokens = count * rows
    seq = lambda cols, dtype=bf16: ((count, rows, cols), dtype)
    kv = [seq(dim)] * 4
    hbm = pl.BlockSpec(memory_space=pl.ANY)
    vmem = pl.BlockSpec(memory_space=pltpu.VMEM)
    stat = ((count, 8, rows), f32)
    outs = [seq(model), seq(model), seq(dim // 2, f32), seq(dim // 2, f32), ((model, tokens), bf16), seq(width)] + kv[:3] + [
        seq(model), seq(width), ((heads, dim, model), f32), stat, stat, ((8, model), f32)]
    scratch = [seq(model), seq(model), (wq.shape, bf16), (wk.shape, bf16), (wv.shape, bf16), (wo.shape, bf16), seq(dim // 2, f32), seq(dim // 2, f32),
               ((model, tokens), bf16), seq(width)] + kv + [seq(width, f32), ((width, tokens), bf16), ((tokens, model), bf16), seq(width),
               ((2, dim, model), f32), ((heads, dim, rows), f32), ((2, 8, rows), f32)]
    sems = [count, count, count, count, 4, 11, 2]
    return pl.pallas_call(
        functools.partial(front_kernel, count, heads),
        name="front",
        in_specs=[hbm, hbm, vmem, vmem, vmem, hbm, hbm, hbm, hbm],
        out_specs=[hbm] * 12 + [vmem] * 3,
        out_shape=[jax.ShapeDtypeStruct(*o) for o in outs],
        scratch_shapes=[pltpu.VMEM(*s) for s in scratch] + [pltpu.SemaphoreType.DMA((n,)) for n in sems],
        compiler_params=pltpu.CompilerParams(collective_id=1, has_side_effects=True, vmem_limit_bytes=67000000),
        cost_estimate=pl.CostEstimate(flops=10 ** 10, bytes_accessed=8 * 2 ** 20, transcendentals=0),
    )(x_in, dy_in, angle, gain_pre, gain_post, wq, wk, wv, wo)


class SumAll:
    def __init__(self, total, out, slots, send, recv, keep, me):
        self.total, self.out, self.send, self.recv, self.keep = total, out, send, recv, keep
        self.from_core, self.from_first, self.from_second = slots
        core, chip = lax.rem(me, 2), me // 2
        self.core = core
        swap = chip + 1 - 2 * lax.rem(chip, 2)
        turn = lax.rem(chip + 3 + 2 * lax.rem(chip, 2), 4)
        low, high = lax.rem((chip + 1) // 2, 2), chip // 2
        self.sibling = me + 1 - 2 * core
        self.first = (swap * 2 + core, turn * 2 + core)
        self.second = (turn * 2 + core, swap * 2 + core)
        self.sub = (low, high)
        self.quarter = (high, low)
        self.base = (core * 8, core * 8 + 4)

    def move(self, start, blocks, target, at_block, sem, device, source=None):
        source = self.total if source is None else source
        return pltpu.make_async_remote_copy(
            src_ref=source.at[pl.ds(start, blocks)], dst_ref=target.at[pl.ds(at_block, blocks)], send_sem=self.send.at[sem],
            recv_sem=self.recv.at[sem], device_id={"cp": device}, device_id_type=MESH)

    def half(self):
        return self.move((1 - self.core) * 8, 8, self.from_core, 0, 0, self.sibling)

    def reduce_first(self, s):
        return self.move(self.base[s] + (1 - self.sub[s]) * 2, 2, self.from_first, 2 * s, 1 + s, self.first[s])

    def reduce_second(self, s):
        return self.move(self.base[s] + self.sub[s] * 2 + 1 - self.quarter[s], 1, self.from_second, s, 3 + s, self.second[s])

    def gather_second(self, s):
        at_block = self.base[s] + self.sub[s] * 2 + self.quarter[s]
        return self.move(at_block, 1, self.out, at_block, 5 + s, self.second[s])

    def keep_own(self, s):
        block = pl.ds(self.base[s] + self.sub[s] * 2 + self.quarter[s], 1)
        return pltpu.make_async_copy(self.total.at[block], self.out.at[block], self.keep.at[s])

    def gather_first(self, s):
        at_block = self.base[s] + self.sub[s] * 2
        return self.move(at_block, 2, self.out, at_block, 7 + s, self.first[s], self.out)

    def share_own(self, s):
        at_block = self.base[s] + self.sub[s] * 2
        return self.move(at_block, 2, self.out, at_block, 9 + s, self.sibling, self.out)

    def share_other(self, s):
        at_block = self.base[s] + (1 - self.sub[s]) * 2
        return self.move(at_block, 2, self.out, at_block, 11 + s, self.sibling, self.out)

    def add(self, start, source, at_block, blocks):
        def body(n, carry):
            self.total[start + n] = self.total[start + n] + source[at_block + n]
            return carry

        lax.fori_loop(0, blocks, body, 0)

    def begin(self):
        self.half().start()

    def finish_half(self):
        self.half().wait_recv()
        for s in range(2):
            self.add(self.base[s] + (1 - self.sub[s]) * 2, self.from_core, s * 4 + (1 - self.sub[s]) * 2, 2)
        for s in range(2):
            self.reduce_first(s).start()
        for s in range(2):
            self.add(self.base[s] + self.sub[s] * 2, self.from_core, s * 4 + self.sub[s] * 2, 2)

    def finish_first(self):
        for s in range(2):
            self.reduce_first(s).wait_recv()
            self.add(self.base[s] + self.sub[s] * 2, self.from_first, 2 * s, 2)
            self.reduce_second(s).start()

    def finish_second(self):
        for s in range(2):
            self.reduce_second(s).wait_recv()
            self.add(self.base[s] + self.sub[s] * 2 + self.quarter[s], self.from_second, s, 1)
            self.gather_second(s).start()
            self.keep_own(s).start()

    def finish_gather(self):
        for s in range(2):
            self.gather_second(s).wait_recv()
            self.keep_own(s).wait()
            self.gather_first(s).start()
            self.share_own(s).start()

    def finish_share(self):
        for s in range(2):
            self.gather_first(s).wait_recv()
            self.share_other(s).start()

    def end(self):
        for s in range(2):
            self.share_own(s).wait_recv()
            self.share_other(s).wait_recv()
        self.half().wait_send()
        for s in range(2):
            for step in (self.reduce_first, self.reduce_second, self.gather_second, self.gather_first, self.share_own, self.share_other):
                step(s).wait_send()


def back_kernel(count, heads, y_in, x_in, dy_in, q_in, do_in, k_in, kt_in, v_in, actt_in, cos_in, sin_in, dwo_in, wq_in, wk_in, wv_in,
                lse, delta, dpost, gain_pre,
                y_out, dx_out, dwo_out, dqkv_out, gains_out,
                x, dy, q, do, k, kt, v, actt, cosine, sine, wqkv, dqkv, dqt, dka, dva, dx, dpre, gains,
                wo_sum, wo_half, wo_first, wo_second, qkv_sum, qkv_half, qkv_first, qkv_second,
                y_send, y_recv, dx_send, dx_recv, gain_send, gain_recv, wo_send, wo_recv, qkv_send, qkv_recv, load_sem, piece_sem, wo_keep, qkv_keep):
    me = lax.axis_index("cp")
    rows, model = x.shape[1:]
    dim = k.shape[-1]
    width = heads * dim
    greet(me, count)
    wo_total = SumAll(wo_sum, dwo_out, (wo_half, wo_first, wo_second), wo_send, wo_recv, wo_keep, me)
    qkv_total = SumAll(qkv_sum, dqkv_out, (qkv_half, qkv_first, qkv_second), qkv_send, qkv_recv, qkv_keep, me)
    y_move = Exchange(y_in, y_out, y_send, y_recv, me, count)
    dx_move = Exchange(dx, dx_out, dx_send, dx_recv, me, count)
    order = [0] + near_first(count)

    def fetch(i, slot):
        return [pltpu.make_async_copy(a.at[i], b.at[slot], piece_sem.at[slot, n]) for n, (a, b) in enumerate(
            ((q_in, q), (do_in, do), (x_in, x), (dy_in, dy)))]

    loads = [pltpu.make_async_copy(a, b, load_sem.at[n]) for n, (a, b) in enumerate((
        (dwo_in, wo_sum), (k_in, k), (kt_in, kt), (v_in, v), (cos_in, cosine), (sin_in, sine),
        (wq_in, wqkv.at[:, 0:width]), (wk_in, wqkv.at[:, width:width + dim]), (wv_in, wqkv.at[:, width + dim:]), (actt_in, actt)))]
    for load in loads:
        load.start()
    for load in fetch(count - 1, 0):
        load.start()
    loads[0].wait()
    wo_total.begin()
    dka[...] = jnp.zeros_like(dka)
    dva[...] = jnp.zeros_like(dva)
    dpre[...] = jnp.zeros_like(dpre)
    for load in loads[1:]:
        load.wait()
    wo_total.finish_half()
    y_move.start(order[:4])

    def step(g, carry):
        i = count - 1 - g
        slot = lax.rem(g, 2)

        @pl.when(g < count - 1)
        def _():
            for load in fetch(i - 1, 1 - slot):
                load.start()

        for load in fetch(i, slot):
            load.wait()
        dqt[...] = jnp.zeros_like(dqt)

        def block(j, masked):
            key, key_t, val = k[j], kt[j], v[j]
            for h in range(heads):
                qh = q[slot, :, h * dim:(h + 1) * dim]
                doh = do[slot, :, h * dim:(h + 1) * dim]
                t = jnp.tanh(dot(key, qh, NT) * (1.0 / SOFT_CAP))
                p = jnp.exp(SOFT_CAP * t - lse[i, h:h + 1, :])
                if masked:
                    allowed = lax.broadcasted_iota(jnp.int32, t.shape, 0) <= lax.broadcasted_iota(jnp.int32, t.shape, 1)
                    p = jnp.where(allowed, p, 0.0)
                dp = dot(val, doh, NT)
                ds = bf(p * (dp - delta[i, h:h + 1, :]) * (1.0 - t * t))
                dva[j] += dot(bf(p), doh)
                dka[j] += dot(ds, qh)
                dqt[h] += dot(key_t, ds)

        def body(j, carry):
            block(j, False)
            return carry

        lax.fori_loop(0, i, body, 0)
        block(i, True)
        c, s = cosine[i], sine[i]
        rws = pl.ds(pl.multiple_of(i * rows, rows), rows)
        for h in range(heads):
            dqkv[rws, h * dim:(h + 1) * dim] = bf(rotate_back(dqt[h].T, c, s) * QUERY_SCALE ** -0.5)
        dqkv[rws, width:width + dim] = bf(rotate_back(dka[i], c, s))
        dqkv[rws, width + dim:] = bf(dva[i])
        da = dot(dqkv[rws, :], wqkv[...], NT)
        du, dgain = norm_grad(x[slot].astype(jnp.float32), gain_pre[...], da)
        dpre[...] += jnp.sum(dgain.reshape(rows // 8, 8, model), axis=0)
        dx[i] = bf(dy[slot].astype(jnp.float32) + du)

        @pl.when(g == 1)
        def _():
            wo_total.finish_first()
            y_move.start(order[4:6])

        @pl.when(g == 3)
        def _():
            wo_total.finish_second()
            y_move.start(order[6:])

        @pl.when(g == 5)
        def _():
            wo_total.finish_gather()

        return carry

    lax.fori_loop(0, count, step, 0)
    dx_move.start(order[-3:])
    part = qkv_sum.shape[1] * 4

    def weight(n, carry):
        at_block = lax.rem((1 - qkv_total.core) * 2 + n, 4)
        lhs = actt[pl.ds(pl.multiple_of(at_block * part, 16), part), :]
        qkv_sum[pl.ds(at_block * 4, 4)] = dot(lhs, dqkv[...]).reshape(4, part // 4, width + 2 * dim)

        @pl.when(n == 1)
        def _():
            qkv_total.begin()
            wo_total.finish_share()

        return carry

    lax.fori_loop(0, 4, weight, 0)
    gains[me] = jnp.concatenate([jnp.sum(dpre[...], axis=0, keepdims=True), jnp.sum(dpost[...], axis=0, keepdims=True), jnp.zeros((6, model), jnp.float32)], axis=0)
    qkv_total.finish_half()
    dx_move.start(order[:2])

    def send_gains(step):
        to = lax.rem(me + step, count)
        return pltpu.make_async_remote_copy(
            src_ref=gains.at[me], dst_ref=gains.at[me], send_sem=gain_send.at[to], recv_sem=gain_recv.at[me], device_id={"cp": to}, device_id_type=MESH)

    for n in range(1, count):
        send_gains(n).start()
    qkv_total.finish_first()
    dx_move.start(order[2:4])
    wo_total.end()
    for n in range(1, count):
        source = lax.rem(me + n, count)
        pltpu.make_async_copy(gains.at[source], gains.at[source], gain_recv.at[source]).wait()
    gains_out[...] = jnp.sum(gains[...], axis=0)
    qkv_total.finish_second()
    dx_move.start(order[4:-3])
    qkv_total.finish_gather()
    qkv_total.finish_share()
    qkv_total.end()
    for n in range(1, count):
        send_gains(n).wait_send()
    for source in range(count):
        dx_move.wait_from(source)
    dx_move.wait_sent()
    for source in range(count):
        y_move.wait_from(source)
    y_move.wait_sent()


def back(count, heads, y, x, dy, q, do, k, kt, v, actt, cosine, sine, dwo, wq, wk, wv, lse, delta, dpost, gain_pre):
    bf16, f32 = jnp.bfloat16, jnp.float32
    _, rows, model = x.shape
    dim = wk.shape[1]
    width = heads * dim
    wide = width + 2 * dim
    tokens = count * rows
    seq = lambda cols, dtype=bf16, n=count: ((n, rows, cols), dtype)
    blocks = lambda n, height, cols: ((n, height // 16, cols), f32)
    hbm = pl.BlockSpec(memory_space=pl.ANY)
    vmem = pl.BlockSpec(memory_space=pltpu.VMEM)
    outs = [seq(model), seq(model), blocks(16, width, model), blocks(16, model, wide), ((8, model), f32)]
    scratch = [seq(model, n=2), seq(model, n=2), seq(width, n=2), seq(width, n=2), seq(dim), seq(dim), seq(dim), (actt.shape, bf16),
               seq(dim // 2, f32), seq(dim // 2, f32), ((model, wide), bf16), ((tokens, wide), bf16), ((heads, dim, rows), f32),
               seq(dim, f32), seq(dim, f32), seq(model), ((8, model), f32), ((count, 8, model), f32)]
    scratch += [blocks(n, width, model) for n in (16, 8, 4, 2)] + [blocks(n, model, wide) for n in (16, 8, 4, 2)]
    sems = [(count,)] * 6 + [(13,)] * 4 + [(10,), (2, 4), (2,), (2,)]
    return pl.pallas_call(
        functools.partial(back_kernel, count, heads),
        name="back",
        in_specs=[hbm] * 15 + [vmem] * 4,
        out_specs=[hbm] * 4 + [vmem],
        out_shape=[jax.ShapeDtypeStruct(*o) for o in outs],
        scratch_shapes=[pltpu.VMEM(*s) for s in scratch] + [pltpu.SemaphoreType.DMA(n) for n in sems],
        compiler_params=pltpu.CompilerParams(collective_id=2, has_side_effects=True, vmem_limit_bytes=67000000),
        cost_estimate=pl.CostEstimate(flops=10 ** 10, bytes_accessed=8 * 2 ** 20, transcendentals=0),
    )(y, x, dy, q, do, k, kt, v, actt, cosine, sine, dwo.reshape(16, width // 16, model), wq, wk, wv, lse, delta, dpost, gain_pre)


def solution(mesh):
    count = mesh.shape["cp"]

    def local_step(x_in, positions, dy_out, w_query, w_key, w_value, w_out, w_pre, w_post):
        model = x_in.shape[-1]
        heads, dim = w_query.shape[1], w_query.shape[2]
        width = heads * dim
        f32 = jnp.float32
        wq = w_query.reshape(model, width)
        wk = w_key.reshape(model, dim)
        wv = w_value.reshape(model, dim)
        wo = w_out.reshape(width, model)
        gain_pre = w_pre.reshape(1, model)
        gain_post = w_post.reshape(1, model)

        pos = lax.all_to_all(positions, "cp", 0, 0, tiled=True)
        inv_freq = ROPE_BASE ** (jnp.arange(dim // 2, dtype=f32) * (-2.0 / dim))
        angle = pos.astype(f32)[:, :, None] * inv_freq
        x, dy, cosine, sine, actt, q, k, kt, v, y, do, dwo, lse, delta, dpost = front(
            count, heads, x_in, dy_out, angle, gain_pre, gain_post, wq, wk, wv, wo)
        y_out, dx_in, dwo, dqkv, gains = back(
            count, heads, y, x, dy, q, do, k, kt, v, actt, cosine, sine, dwo, wq, wk, wv, lse, delta, dpost, gain_pre)
        width = heads * dim
        dqkv = dqkv.reshape(model, width + 2 * dim)
        return (y_out, dx_in, dqkv[:, :width].reshape(model, heads, dim), dqkv[:, None, width:width + dim], dqkv[:, None, width + dim:],
                dwo.reshape(heads, dim, model), gains[0], gains[1])

    seq_spec = P("dp", "cp", None)
    in_specs = (seq_spec, P("dp", "cp"), seq_spec, P(), P(), P(), P(), P(), P())
    out_specs = (seq_spec, seq_spec, P("dp", None, None), P("dp", None, None), P("dp", None, None), P("dp", None, None), P("dp"), P("dp"))
    return jax.shard_map(local_step, mesh=mesh, in_specs=in_specs, out_specs=out_specs, check_vma=False)
```

profile of v0, /device:TPU:81, one launch (start us, length us, event | category | flops | bytes accessed | tf_op | source)
XLA Modules:
  0.0 391.7 jit_solution(15642058032040629526)
XLA Ops:
  0.6 1.3 all_to_all.6
  1.9 6.0 %all-to-all-start = ((s32[8,1,256]{2,1,0:T(1,128)}), s32[8,1,256]{2,1,0:T(1,128)S(1)}, u32[]{:S(2)}, u32[]{:S(2)}) async-start(s32[8,1,256]{2,1,0:T(1,128)} %all_to_all.6), calls=%async_computation | async-start | bytes 16384 | tf_op jit(solution)/shard_map/all_to_all | solution.py:587
  8.0 1.3 reshape.59.gain_pre
  9.3 1.3 reshape.60.gain_post
  10.6 3.6 copy.18
  14.2 0.0 all-to-all-done
  14.2 1.3 broadcast_multiply_fusion.angle
  15.5 124.4 %front.1 = (bf16[8,256,1152]{2,1,0:T(8,128)(2,1)}, bf16[8,256,1152]{2,1,0:T(8,128)(2,1)}, f32[8,256,128]{2,1,0:T(8,128)}, f32[8,256,128]{2,1,0:T(8,128)}, bf16[1...) custom-call(bf16[8,256,1152]{2,1,0:T(8,128)(2,1)} %x_in.1, ...), custom_call_target="tpu_custom_call" | custom-call | flops 10000000000 | bytes 8388608 | tf_op jit(solution)/shard_map/front/pallas_call | solution.py:276
  139.9 223.8 %back.1 = (bf16[8,256,1152]{2,1,0:T(8,128)(2,1)}, bf16[8,256,1152]{2,1,0:T(8,128)(2,1)}, f32[16,64,1152]{2,1,0:T(8,128)}, f32[16,72,1536]{2,1,0:T(8,128)}, f32[8,1152]{1,0:T(8,128)}) custom-call(bf16[8,256,1152]{2,1,0:T(8,128)(2,1)} %get-tuple-element.28.y_in, bf16[8,256,1152]{2,1,0:T(8,128)(2,1)} %get-tuple-element.29.x_in, ...), custom_call_target="tpu_custom_call" | custom-call | flops 10000000000 | bytes 8388608 | tf_op jit(solution)/shard_map/back/pallas_call | solution.py:560
  363.8 1.8 fusion
  365.6 5.2 %slice.20 = f32[1152,1024]{1,0:T(8,128)} slice(f32[1152,1536]{1,0:T(8,128)} %bitcast.14), slice={[0:1152], [0:1024]} | slice | bytes 9437184 | tf_op jit(solution)/shard_map/slice | solution.py:596
  370.8 1.5 slice_reduce_fusion
  372.3 0.0 slice-start.2
  372.3 6.7 %reshape.67 = f32[1152,4,256]{2,1,0:T(4,128)} reshape(f32[1152,1024]{1,0:T(8,128)} %slice.20) | data formatting | bytes 9437184 | tf_op jit(solution)/shard_map/reshape | solution.py:596
  379.0 1.6 broadcast_in_dim.9
  380.6 0.0 slice-start.3
  380.6 1.6 broadcast_in_dim.8
  382.3 0.0 slice-start
  382.3 5.0 %copy.24 = bf16[8,256,1152]{2,1,0:T(8,128)(2,1)} copy(bf16[8,256,1152]{2,1,0:T(8,128)(2,1)} %get-tuple-element.60) | data formatting | bytes 9437184
  387.3 0.0 slice-done.2
  387.3 0.0 slice-done.3
  387.3 0.0 slice-start.1
  387.3 2.2 copy.25
  389.5 0.0 slice-done
  389.5 0.0 slice-done.1
  389.5 2.2 copy.26
  (5 shorter events, 0.0 us)
Async XLA Ops:
  1.9 12.3 %all-to-all-start = ((s32[8,1,256]{2,1,0:T(1,128)}), s32[8,1,256]{2,1,0:T(1,128)S(1)}, u32[]{:S(2)}, u32[]{:S(2)}) async-start(s32[8,1,256]{2,1,0:T(1,128)} %all_to_all.6), calls=%async_computation | async-start | bytes 16384 | tf_op jit(solution)/shard_map/all_to_all | solution.py:587
  372.3 15.0 %slice-start.2 = ((s8[4718592]{0:T(1024)(128)(4,1)}), s8[524288]{0:T(1024)(128)(4,1)S(1)}, s32[]{:S(2)}) async-start(s8[4718592]{0:T(1024)(128)(4,1)} %bitcast.18), calls=%async_computation.3 | async-start | bytes 1048576
  380.6 6.7 %slice-start.3 = ((s8[4718592]{0:T(1024)(128)(4,1)}), s8[4194304]{0:T(1024)(128)(4,1)S(1)}, s32[]{:S(2)}) async-start(s8[4718592]{0:T(1024)(128)(4,1)} %bitcast.18), calls=%async_computation.4 | async-start | bytes 8388608
  382.3 7.2 %slice-start = ((s8[4718592]{0:T(1024)(128)(4,1)}), s8[4194304]{0:T(1024)(128)(4,1)S(1)}, s32[]{:S(2)}) async-start(s8[4718592]{0:T(1024)(128)(4,1)} %bitcast.15), calls=%async_computation.1 | async-start | bytes 8388608
  387.3 2.2 slice-start.1
where the time goes:
time: 392 us
  Pallas kernels  348 us (89%)
  local copies, waits for them, and re-layouts  35.4 us (9%)
  starting transfers between devices  6.01 us (2%)
    pallas_call x1, Pallas kernels, back(): pl.pallas_call(functools.partial(back_kernel, count, heads), name='back',...  224 us
    pallas_call x1, Pallas kernels, front(): pl.pallas_call(functools.partial(front_kernel, count, heads), name='front...  124 us
    unnamed x13, local copies, waits for them, and re-layouts  13.1 us
  transfers between devices with their start and end apart: 1, of which 0 were waited for; matrix products, arithmetic and copies ran while one was open for 2% of the time, Pallas kernels for 0%

commit v1 on v0

--- a/solution.py
+++ b/solution.py
@@ -168,8 +168,8 @@
         stat[0] = jnp.full(stat.shape[1:], -1e30, jnp.float32)
         stat[1] = jnp.zeros(stat.shape[1:], jnp.float32)
 
-        def block(j, masked):
-            key, val_t = k[j], vt[j]
+        def block(j, masked, wide=1):
+            key = k[pl.ds(j, wide)].reshape(wide * rows, dim)
             for h in range(heads):
                 s = dot(key, q[i, :, h * dim:(h + 1) * dim], NT)
                 c = SOFT_CAP * jnp.tanh(s * (1.0 / SOFT_CAP))
@@ -182,13 +182,22 @@
                 p = jnp.exp(c - new)
                 stat[1, h:h + 1, :] = stat[1, h:h + 1, :] * scale + jnp.sum(p, axis=0, keepdims=True)
                 stat[0, h:h + 1, :] = new
-                acc[h] = acc[h] * scale + dot(val_t, bf(p))
+                p = bf(p)
+                out_t = dot(vt[j], p[:rows])
+                for n in range(1, wide):
+                    out_t = out_t + dot(vt[j + n], p[n * rows:(n + 1) * rows])
+                acc[h] = acc[h] * scale + out_t
 
         def body(j, carry):
-            block(j, False)
+            block(2 * j, False, 2)
             return carry
 
-        lax.fori_loop(0, i, body, 0)
+        lax.fori_loop(0, i // 2, body, 0)
+
+        @pl.when(lax.rem(i, 2) == 1)
+        def _():
+            block(i - 1, False)
+
         block(i, True)
         lse_out[i] = stat[0] + jnp.log(stat[1])
         parts = []
@@ -569,6 +578,27 @@
     )(y, x, dy, q, do, k, kt, v, actt, cosine, sine, dwo.reshape(16, width // 16, model), wq, wk, wv, lse, delta, dpost, gain_pre)
 
 
+def finish_kernel(y, dx, dwo, y_out, dx_out, dwo_out):
+    y_out[...] = y[...]
+    dx_out[...] = dx[...]
+    dwo_out[...] = dwo[...]
+
+
+def finish(count, y, dx, dwo):
+    dwo = dwo.reshape(count, -1, dwo.shape[-1])
+    specs = [pl.BlockSpec((1,) + a.shape[1:], lambda i: (i, 0, 0)) for a in (y, dx, dwo)]
+    return pl.pallas_call(
+        finish_kernel,
+        name="finish",
+        grid=(count,),
+        in_specs=specs,
+        out_specs=specs,
+        out_shape=[jax.ShapeDtypeStruct(a.shape, a.dtype) for a in (y, dx, dwo)],
+        compiler_params=pltpu.CompilerParams(dimension_semantics=("arbitrary",)),
+        cost_estimate=pl.CostEstimate(flops=10 ** 8, bytes_accessed=8 * 2 ** 20, transcendentals=0),
+    )(y, dx, dwo)
+
+
 def solution(mesh):
     count = mesh.shape["cp"]
 
@@ -591,6 +621,7 @@
             count, heads, x_in, dy_out, angle, gain_pre, gain_post, wq, wk, wv, wo)
         y_out, dx_in, dwo, dqkv, gains = back(
             count, heads, y, x, dy, q, do, k, kt, v, actt, cosine, sine, dwo, wq, wk, wv, lse, delta, dpost, gain_pre)
+        y_out, dx_in, dwo = finish(count, y_out, dx_in, dwo)
         width = heads * dim
         dqkv = dqkv.reshape(model, width + 2 * dim)
         return (y_out, dx_in, dqkv[:, :width].reshape(model, heads, dim), dqkv[:, None, width:width + dim], dqkv[:, None, width + dim:],

time: 392 us -> 389 us (level)
  local copies, waits for them, and re-layouts: 35.4 us -> 26 us
  Pallas kernels: 348 us -> 355 us
    pallas_call x0 -> x1, Pallas kernels: none -> 12.1 us  [finish(): pl.pallas_call(finish_kernel, name='finish', grid=(count,), in_specs=spec...]
    unnamed x13 -> x2, local copies, waits for them, and re-layouts: 13.1 us -> 3.63 us
    pallas_call x1, Pallas kernels: 124 us -> 119 us  [front(): pl.pallas_call(functools.partial(front_kernel, count, heads), name='front...]
where the time goes in v1:
time: 389 us
  Pallas kernels  355 us (91%)
  local copies, waits for them, and re-layouts  26 us (7%)
  starting transfers between devices  6.01 us (2%)
    pallas_call x1, Pallas kernels, back(): pl.pallas_call(functools.partial(back_kernel, count, heads), name='back',...  223 us
    pallas_call x1, Pallas kernels, front(): pl.pallas_call(functools.partial(front_kernel, count, heads), name='front...  119 us
    pallas_call x1, Pallas kernels, finish(): pl.pallas_call(finish_kernel, name='finish', grid=(count,), in_specs=spec...  12.1 us
  transfers between devices with their start and end apart: 1, of which 0 were waited for; matrix products, arithmetic and copies ran while one was open for 2% of the time, Pallas kernels for 0%

profile of v1, /device:TPU:81, one launch (start us, length us, event | category | flops | bytes accessed | tf_op | source)
XLA Modules:
  0.0 388.6 jit_solution(7924007502765722883)
XLA Ops:
  0.6 1.3 all_to_all.6
  1.9 6.0 %all-to-all-start = ((s32[8,1,256]{2,1,0:T(1,128)}), s32[8,1,256]{2,1,0:T(1,128)S(1)}, u32[]{:S(2)}, u32[]{:S(2)}) async-start(s32[8,1,256]{2,1,0:T(1,128)} %all_to_all.6), calls=%async_computation | async-start | bytes 16384 | tf_op jit(solution)/shard_map/all_to_all | solution.py:617
  8.0 1.3 reshape.62.gain_pre
  9.3 1.3 reshape.63.gain_post
  10.6 3.6 copy.18
  14.2 0.0 all-to-all-done
  14.2 1.3 broadcast_multiply_fusion.angle
  15.5 119.2 %front.1 = (bf16[8,256,1152]{2,1,0:T(8,128)(2,1)}, bf16[8,256,1152]{2,1,0:T(8,128)(2,1)}, f32[8,256,128]{2,1,0:T(8,128)}, f32[8,256,128]{2,1,0:T(8,128)}, bf16[1...) custom-call(bf16[8,256,1152]{2,1,0:T(8,128)(2,1)} %x_in.1, ...), custom_call_target="tpu_custom_call" | custom-call | flops 10000000000 | bytes 8388608 | tf_op jit(solution)/shard_map/front/pallas_call | solution.py:285
  134.7 223.4 %back.1 = (bf16[8,256,1152]{2,1,0:T(8,128)(2,1)}, bf16[8,256,1152]{2,1,0:T(8,128)(2,1)}, f32[16,64,1152]{2,1,0:T(8,128)}, f32[16,72,1536]{2,1,0:T(8,128)}, f32[8,1152]{1,0:T(8,128)}) custom-call(bf16[8,256,1152]{2,1,0:T(8,128)(2,1)} %get-tuple-element.31.y_in, bf16[8,256,1152]{2,1,0:T(8,128)(2,1)} %get-tuple-element.32.x_in, ...), custom_call_target="tpu_custom_call" | custom-call | flops 10000000000 | bytes 8388608 | tf_op jit(solution)/shard_map/back/pallas_call | solution.py:569
  358.1 1.8 fusion
  359.9 5.2 %slice.20 = f32[1152,1024]{1,0:T(8,128)} slice(f32[1152,1536]{1,0:T(8,128)} %bitcast.15), slice={[0:1152], [0:1024]} | slice | bytes 9437184 | tf_op jit(solution)/shard_map/slice | solution.py:627
  365.1 1.5 slice_reduce_fusion
  366.6 6.7 %reshape.71 = f32[1152,4,256]{2,1,0:T(4,128)} reshape(f32[1152,1024]{1,0:T(8,128)} %slice.20) | data formatting | bytes 9437184 | tf_op jit(solution)/shard_map/reshape | solution.py:627
  373.2 1.6 broadcast_in_dim.9
  374.9 1.6 broadcast_in_dim.8
  376.5 12.1 %finish.1 = (bf16[8,256,1152]{2,1,0:T(8,128)(2,1)}, bf16[8,256,1152]{2,1,0:T(8,128)(2,1)}, f32[8,128,1152]{2,1,0:T(8,128)}) custom-call(bf16[8,256,1152]{2,1,0:T(8,128)(2,1)} %get-tuple-element.46.y, bf16[8,256,1152]{2,1,0:T(8,128)(2,1)} %get-tuple-element.47.dx, f32[8,128,1152]{2,1,0:T(8,128)} %bitcast.16), custom_call_target="tpu_custom_call" | custom-call | flops 100000000 | bytes 8388608 | tf_op jit(solution)/shard_map/finish/pallas_call | solution.py:590
  (3 shorter events, 0.0 us)
Async XLA Ops:
  1.9 12.3 %all-to-all-start = ((s32[8,1,256]{2,1,0:T(1,128)}), s32[8,1,256]{2,1,0:T(1,128)S(1)}, u32[]{:S(2)}, u32[]{:S(2)}) async-start(s32[8,1,256]{2,1,0:T(1,128)} %all_to_all.6), calls=%async_computation | async-start | bytes 16384 | tf_op jit(solution)/shard_map/all_to_all | solution.py:617
